TPU v7x, 32 devices: a whole 2x2x4 slice. The times are simulated.
32 devices in a mesh: arcs: 8 (over y, x, core), tiles: 4 (over z).
Axes of the slice: x: 2, y: 2, z: 4, core: 2. Of those that a mesh axis runs over, the one named last changes fastest.
Arguments:
- design: bfloat16 [12288, 8192], P('arcs', 'tiles'), may hold values from -0.09375 to 0.09375
- observations: float32 [12288], P('arcs'), may hold values from -25 to 25
- solution: float32 [8192], P('tiles'), may hold values from -6 to 6
- arc_ids: int32 [8, 1536], P('arcs'), may hold values from 0 to 3, never falling along the last dimension, each value on 1 to 768 neighbouring positions
- block_live: int32 [8, 12], P('arcs'), may hold values 0 or 1
Outputs:
- normal: float32 [8192, 8192], P('arcs', 'tiles')
- rhs: float32 [8192], P('tiles')
Inputs may be any that keep to these rules, and one draw needn't show every extreme that they name: `arc_ids`: the arcs of a group's rows never fall along its rows; an arc holds at most 768 rows and some arc exactly that many.
All inputs are finite; a program needn't handle non-finite values. No bound on the sum of `block_live` on one device may be relied on, other than what follows from the above.
Results may differ from a plain program's by a relative error of at most 0.0018.
Values may be sent and summed in bfloat16 or wider, within the bound.
A program may use at most 192 MiB of HBM per device.

v0:
```python
import jax
import jax.numpy as jnp
from jax import lax
from jax.sharding import PartitionSpec as P

ARCS_DEV = 4
prior_rows = 4.0


def contract_rows(left, right):
    return lax.dot_general(
        left, right, (((0,), (0,)), ((), ())), preferred_element_type=jnp.float32
    )


def local(design, observations, solution, arc_ids, block_live):
    row_count = design.shape[0]
    design_all = lax.all_gather(design, "tiles", axis=1, tiled=True)
    partial_value = jnp.dot(design.astype(jnp.float32), solution, precision=lax.Precision.HIGHEST)
    predicted = lax.psum(partial_value, "tiles")
    residual = observations - predicted
    live_row = (
        jnp.broadcast_to(block_live[0][:, None], (block_live.shape[1], 128))
        .reshape(row_count)
        .astype(jnp.float32)
    )
    arc_match = (arc_ids[0][None, :] == jnp.arange(ARCS_DEV, dtype=jnp.int32)[:, None]).astype(
        jnp.float32
    )
    squares = live_row * residual * residual
    arc_squares = jnp.sum(arc_match * squares[None, :], axis=1)
    arc_counts = jnp.sum(arc_match * live_row[None, :], axis=1)
    totals = lax.psum((jnp.sum(arc_squares), jnp.sum(arc_counts)), "arcs")
    variance_all = (totals[0] + 1.0) / (totals[1] + 1.0)
    arc_weight = variance_all / (
        (arc_squares + prior_rows * variance_all) / (arc_counts + prior_rows)
    )
    row_weight = live_row * jnp.sum(arc_match * arc_weight[:, None], axis=0)
    rhs_part = lax.dot_general(
        design.astype(jnp.float32),
        row_weight * residual,
        (((0,), (0,)), ((), ())),
        precision=lax.Precision.HIGHEST,
    )
    weighted = (row_weight[:, None] * design).astype(jnp.bfloat16)
    normal = lax.psum_scatter(
        contract_rows(design_all, weighted), "arcs", scatter_dimension=0, tiled=True
    )
    rhs = lax.psum(rhs_part, "arcs")
    return (normal, rhs)


def solution(mesh):
    return jax.shard_map(
        local,
        mesh=mesh,
        in_specs=(P("arcs", "tiles"), P("arcs"), P("tiles"), P("arcs", None), P("arcs", None)),
        out_specs=(P("arcs", "tiles"), P("tiles")),
        check_vma=False,
    )
```

profile of v0, /device:TPU:0, one launch (start us, length us, event | category | flops | bytes accessed | tf_op | source)
XLA Modules:
  0.0 898.4 jit_solution(16531943414175356195)
XLA Ops:
  7.2 0.0 copy-start
  7.2 0.0 copy-start.2
  7.2 0.0 copy-start.1
  7.2 0.0 all-gather.2.cloned.1.call-start
  7.2 0.7 all-gather.2.cloned.1.call-update
  7.9 0.0 reduce-scatter.2.cloned.1.call-start
  8.0 0.7 reduce.2
  8.7 0.0 copy-done
  8.7 7.0 convolution_reduce_fusion
  15.7 13.7 %psum.28 = f32[1536]{0:T(1024)S(1)} all-reduce(f32[1536]{0:T(1024)S(1)} %convolution_reduce_fusion), channel_id=1, replica_groups=mesh['arcs'=8,'tiles'=4] {'tiles'}, use_global_device_ids=true, to_apply=%region_0.0 | all-reduce | flops 1536 | bytes 12288 | tf_op jit(solution)/shard_map/psum | solution.py:20
  29.5 0.0 copy-done.2
  29.5 0.1 broadcast_bitcast_fusion
  29.6 0.0 copy-done.1
  29.6 0.1 multiply_multiply_fusion
  29.6 0.6 select_reduce_fusion.1
  30.3 13.2 %all-reduce = (f32[]{:T(128)}, f32[]{:T(128)}) all-reduce(f32[]{:T(128)} %get-tuple-element.11, f32[]{:T(128)} %get-tuple-element.6), channel_id=1, replica_groups=mesh['arcs'=8,'tiles'=4] {'arcs'}, use_global_device_ids=true, to_apply=%region_2.0 | all-reduce | flops 2 | bytes 16 | tf_op jit(solution)/shard_map/psum | solution.py:33
  44.9 0.1 select_reduce_fusion.4
  45.0 0.1 fusion.1
  45.0 392.5 %all-gather.2.cloned.1.call-done = bf16[1536,8192]{1,0:T(8,128)(2,1)} async-done(((bf16[1536,2048]{1,0:T(8,128)(2,1)}), bf16[1536,8192]{1,0:T(8,128)(2,1)}) %all-gather.2.cloned.1.call-update) | async-done | bytes 25165840 | tf_op jit(solution)/shard_map/all_gather | solution.py:18
  437.5 62.7 %convolution_bitcast_fusion = f32[8192,2048]{0,1:T(8,128)} fusion(bf16[1536,8192]{1,0:T(8,128)(2,1)} %all-gather.2.cloned.1.call-done, bf16[1536,2048]{1,0:T(8,128)(2,1)} %param.5, f32[1536]{0:T(1024)S(1)} %get-tuple-element.15), kind=kOutput, calls=%fused_computation | convolution fusion | flops 51549044736 | bytes 98572288 | tf_op jit(solution)/shard_map/dot_general | solution.py:11
  500.2 0.0 reduce-scatter.2.cloned.1.call-update
  500.3 4.6 fusion.2
  504.8 14.6 %psum.31 = f32[2048]{0:T(1024)} all-reduce(f32[2048]{0:T(1024)S(1)} %bitcast.19), channel_id=1, replica_groups=mesh['arcs'=8,'tiles'=4] {'arcs'}, use_global_device_ids=true, to_apply=%region_9.0 | all-reduce | flops 2048 | bytes 16384 | tf_op jit(solution)/shard_map/psum | solution.py:49
  519.5 363.0 %reduce-scatter.2.cloned.1.call-done = f32[1024,2048]{0,1:T(8,128)} async-done(((f32[8192,2048]{0,1:T(8,128)}), f32[1024,2048]{0,1:T(8,128)}) %reduce-scatter.2.cloned.1.call-update) | async-done | bytes 8388624 | tf_op jit(solution)/shard_map/reduce_scatter | solution.py:46
  882.4 9.1 %copy.8 = f32[1024,2048]{1,0:T(8,128)} copy(f32[1024,2048]{0,1:T(8,128)} %reduce-scatter.2.cloned.1.call-done) | data formatting | bytes 16777216
  (3 shorter events, 0.0 us)
Async XLA Ops:
  7.2 1.5 copy-start
  7.2 22.3 %copy-start.2 = (s32[1,12]{1,0:T(1,128)S(1)}, s32[1,12]{1,0:T(1,128)}, u32[]{:S(2)}) copy-start(s32[1,12]{1,0:T(1,128)} %param.9) | copy-start | bytes 148
  7.2 22.4 %copy-start.1 = (f32[1536]{0:T(1024)S(1)}, f32[1536]{0:T(1024)}, u32[]{:S(2)}) copy-start(f32[1536]{0:T(1024)} %param.6) | copy-start | bytes 18436
  7.2 430.3 %all-gather.2.cloned.1.call-start = ((), (), s32[]{:S(2)}) async-start(), calls=%async_computation.1 | async-start | bytes 31457280 | tf_op jit(solution)/shard_map/all_gather | solution.py:18
  7.9 874.5 %reduce-scatter.2.cloned.1.call-start = ((), (), s32[]{:S(2)}) async-start(), calls=%async_computation.2 | async-start | bytes 75497472 | tf_op jit(solution)/shard_map/reduce_scatter | solution.py:46
Sparse Core Ops, SparseCore 0:
  9.6 427.8 all-gather.1
  500.4 381.9 reduce-scatter.1
where the time goes:
time: 899 us; the launch traced here: 898 us
  waiting for transfers between devices  756 us (84%)
  matrix products  74.3 us (8%)
  blocking collectives  41.6 us (5%)
  between operations  15.5 us (2%)
  local copies, waits for them, and re-layouts  9.22 us (1%)
    all_gather x1, waiting for transfers between devices, local(): design_all = lax.all_gather(design, 'tiles', axis=1, tiled=True)  392 us
    reduce_scatter x1, waiting for transfers between devices, local(): lax.psum_scatter(contract_rows(design_all, weighted), 'arcs', scatter_dim...  363 us
    dot_general x1, matrix products, contract_rows(): lax.dot_general(left, right, (((0,), (0,)), ((), ())), preferred_element_...  62.7 us
  transfers between devices with their start and end apart: 2, of which 2 were waited for; matrix products, arithmetic and copies ran while one was open for 1% of the time, Pallas kernels for 0%

commit v1 on v0

--- a/solution.py
+++ b/solution.py
@@ -15,7 +15,8 @@
 
 def local(design, observations, solution, arc_ids, block_live):
     row_count = design.shape[0]
-    design_all = lax.all_gather(design, "tiles", axis=1, tiled=True)
+    sent = jnp.stack([design] * lax.axis_size("tiles"))
+    design_all = jnp.concatenate(lax.all_to_all(sent, "tiles", 0, 0), axis=1)
     partial_value = jnp.dot(design.astype(jnp.float32), solution, precision=lax.Precision.HIGHEST)
     predicted = lax.psum(partial_value, "tiles")
     residual = observations - predicted

time: 899 us -> 1060 us (1.18)
  blocking collectives: 41.6 us -> 433 us
  waiting for transfers between devices: 756 us -> 497 us
  local copies, waits for them, and re-layouts: 9.22 us -> 28.6 us
    all_gather x1 -> x0, waiting for transfers between devices: 392 us -> none  [local(): design_all = lax.all_gather(design, 'tiles', axis=1, tiled=True)]
    psum x1, blocking collectives: 13.7 us -> 405 us  [local(): predicted = lax.psum(partial_value, 'tiles')]
    all_to_all x0 -> x1, waiting for transfers between devices: none -> 116 us  [local(): design_all = jnp.concatenate(lax.all_to_all(sent, 'tiles', 0, 0), axis=1)]
    reduce_scatter x1, waiting for transfers between devices: 363 us -> 381 us  [local(): lax.psum_scatter(contract_rows(design_all, weighted), 'arcs', scatter_dim...]
    another operation x0 -> x1, local copies, waits for them, and re-layouts: none -> 10.7 us  [local(): sent = jnp.stack([design] * lax.axis_size('tiles'))]
where the time goes in v1:
time: 1060 us
  waiting for transfers between devices  497 us (47%)
  blocking collectives  433 us (41%)
  matrix products  75.8 us (7%)
  local copies, waits for them, and re-layouts  28.6 us (3%)
  between operations  15.5 us (1%)
    psum x1, blocking collectives, local(): predicted = lax.psum(partial_value, 'tiles')  405 us
    reduce_scatter x1, waiting for transfers between devices, local(): lax.psum_scatter(contract_rows(design_all, weighted), 'arcs', scatter_dim...  381 us
    all_to_all x1, waiting for transfers between devices, local(): design_all = jnp.concatenate(lax.all_to_all(sent, 'tiles', 0, 0), axis=1)  116 us
    dot_general x1, matrix products, contract_rows(): lax.dot_general(left, right, (((0,), (0,)), ((), ())), preferred_element_...  64.3 us
  transfers between devices with their start and end apart: 2, of which 2 were waited for; matrix products, arithmetic and copies ran while one was open for 1% of the time, Pallas kernels for 0%

profile of v1, /device:TPU:0, one launch (start us, length us, event | category | flops | bytes accessed | tf_op | source)
XLA Modules:
  0.0 1059.4 jit_solution(6140893146219128108)
XLA Ops:
  7.2 0.0 copy-start
  7.2 8.6 copy.10
  15.8 10.7 %stack.2 = bf16[4,1536,2048]{1,2,0:T(8,128)(2,1)} broadcast(bf16[1536,2048]{0,1:T(8,128)(2,1)} %copy.10), dimensions={1,2} | broadcast | bytes 31457280 | tf_op jit(solution)/shard_map/stack | solution.py:18
  26.5 0.0 copy-start.3
  26.5 8.6 all-to-all-start
  35.1 0.0 copy-start.4
  35.1 0.0 copy-start.2
  35.1 0.0 reduce-scatter.2.cloned.1.call-start
  35.2 0.0 copy-done.3
  35.2 0.0 copy-done
  35.2 7.0 convolution_reduce_fusion
  42.2 404.9 %psum.28 = f32[1536]{0:T(1024)S(1)} all-reduce(f32[1536]{0:T(1024)S(1)} %convolution_reduce_fusion), channel_id=1, replica_groups=mesh['arcs'=8,'tiles'=4] {'tiles'}, use_global_device_ids=true, to_apply=%region_0.0 | all-reduce | flops 1536 | bytes 12288 | tf_op jit(solution)/shard_map/psum | solution.py:21
  447.1 0.0 copy-done.4
  447.2 0.1 broadcast_bitcast_fusion
  447.2 0.0 copy-done.2
  447.2 0.1 multiply_multiply_fusion
  447.3 0.6 select_reduce_fusion.1
  447.9 14.1 %all-reduce = (f32[]{:T(128)}, f32[]{:T(128)}) all-reduce(f32[]{:T(128)} %get-tuple-element.13, f32[]{:T(128)} %get-tuple-element.8), channel_id=1, replica_groups=mesh['arcs'=8,'tiles'=4] {'arcs'}, use_global_device_ids=true, to_apply=%region_2.0 | all-reduce | flops 2 | bytes 16 | tf_op jit(solution)/shard_map/psum | solution.py:34
  463.4 0.1 select_reduce_fusion.4
  463.5 0.1 fusion.1
  463.5 116.4 %all-to-all-done = bf16[4,1536,2048]{1,2,0:T(8,128)(2,1)} async-done(((bf16[4,1536,2048]{1,2,0:T(8,128)(2,1)}), bf16[4,1536,2048]{1,2,0:T(8,128)(2,1)}, u32[]{:S(2)}, u32[]{:S(2)}) %all-to-all-start) | async-done | bytes 25165856 | tf_op jit(solution)/shard_map/all_to_all | solution.py:19
  579.9 64.3 %convolution_bitcast_fusion = f32[8192,2048]{0,1:T(8,128)} fusion(bf16[1536,8192]{0,1:T(8,128)(2,1)} %bitcast.4, bf16[1536,2048]{1,0:T(8,128)(2,1)} %param.5, f32[1536]{0:T(1024)S(1)} %get-tuple-element.17), kind=kOutput, calls=%fused_computation | convolution fusion | flops 51549044736 | bytes 98572288 | tf_op jit(solution)/shard_map/dot_general | solution.py:11
  644.2 0.0 reduce-scatter.2.cloned.1.call-update
  644.2 4.6 fusion.2
  648.8 0.0 copy-start.1
  648.8 13.7 %psum.31 = f32[2048]{0:T(1024)} all-reduce(f32[2048]{0:T(1024)S(1)} %bitcast.22), channel_id=1, replica_groups=mesh['arcs'=8,'tiles'=4] {'arcs'}, use_global_device_ids=true, to_apply=%region_9.0 | all-reduce | flops 2048 | bytes 16384 | tf_op jit(solution)/shard_map/psum | solution.py:50
  662.5 380.9 %reduce-scatter.2.cloned.1.call-done = f32[1024,2048]{0,1:T(8,128)} async-done(((f32[8192,2048]{0,1:T(8,128)}), f32[1024,2048]{0,1:T(8,128)}) %reduce-scatter.2.cloned.1.call-update) | async-done | bytes 8388624 | tf_op jit(solution)/shard_map/reduce_scatter | solution.py:47
  1043.4 9.1 copy.11
  1052.5 0.0 copy-done.1
  (4 shorter events, 0.0 us)
Async XLA Ops:
  7.2 28.1 %copy-start = (f32[2048]{0:T(1024)S(1)}, f32[2048]{0:T(1024)}, u32[]{:S(2)}) copy-start(f32[2048]{0:T(1024)} %param.7) | copy-start | bytes 24580
  26.5 8.7 copy-start.3
  26.5 553.4 %all-to-all-start = ((bf16[4,1536,2048]{1,2,0:T(8,128)(2,1)}), bf16[4,1536,2048]{1,2,0:T(8,128)(2,1)}, u32[]{:S(2)}, u32[]{:S(2)}) async-start(bf16[4,1536,2048]{1,2,0:T(8,128)(2,1)} %stack.2), calls=%async_computation | async-start | bytes 50331648 | tf_op jit(solution)/shard_map/all_to_all | solution.py:19
  35.1 412.0 %copy-start.4 = (s32[1,12]{1,0:T(1,128)S(1)}, s32[1,12]{1,0:T(1,128)}, u32[]{:S(2)}) copy-start(s32[1,12]{1,0:T(1,128)} %param.9) | copy-start | bytes 148
  35.1 412.1 %copy-start.2 = (f32[1536]{0:T(1024)S(1)}, f32[1536]{0:T(1024)}, u32[]{:S(2)}) copy-start(f32[1536]{0:T(1024)} %param.6) | copy-start | bytes 18436
  35.1 1008.3 %reduce-scatter.2.cloned.1.call-start = ((), (), s32[]{:S(2)}) async-start(), calls=%async_computation.2 | async-start | bytes 75497472 | tf_op jit(solution)/shard_map/reduce_scatter | solution.py:47
  648.8 403.7 %copy-start.1 = (f32[2048]{0:T(1024)S(1)}, f32[2048]{0:T(1024)}, u32[]{:S(2)}) copy-start(f32[2048]{0:T(1024)} %param.7) | copy-start | bytes 24580
Sparse Core Ops, SparseCore 0:
  644.3 399.0 reduce-scatter.1
